TPU v7x, 32 devices: a whole 2x2x4 slice. The times are simulated.
32 devices in a mesh: dp: 2 (over x), mode: 4 (over z), tm: 4 (over y, core).
Axes of the slice: x: 2, y: 2, z: 4, core: 2. Of those that a mesh axis runs over, the one named last changes fastest.
Arguments:
- input_field: float32 [2, 16, 8, 16384], P(None, 'dp', 'mode', 'tm'), parts along dimension 1, may hold values from -6 to 6
- target_field: float32 [2, 16, 8, 16384], P(None, 'dp', 'mode', 'tm'), parts along dimension 1, may hold values from -6 to 6
- margin: float32 [8, 8, 16], P('mode'), may hold values from -0.5 to 0.5
- pair_index: int32 [16, 2], replicated, may hold values from 0 to 7
- mode_beta: float32 [1024, 8, 3], P(None, 'mode'), may hold values from -2 to 2
- segment_kind: int32 [1], replicated, may hold values from 0 to 1023
Outputs:
- field_gradient: float32 [2, 16, 8, 16384], P(None, 'dp', 'mode', 'tm'), parts along dimension 1
There are 2 independent parts, one for each index of `dp`. A program takes and returns all parts, laid end to end along the dimension named above; an argument that names none is the same for every part. Nothing has to cross between parts.
All inputs are finite; a program needn't handle non-finite values.
Results may differ from a plain program's by a relative error of at most 0.00011.
Values sent between devices are 32-bit elements; how exact they have to be, the bound alone decides.
A program may use at most 128 MiB of HBM per device.

v0:
```python
import functools
import math

import jax
import jax.numpy as jnp
import numpy as np
from jax import lax
from jax.experimental import pallas as pl
from jax.experimental.pallas import tpu as pltpu
from jax.sharding import PartitionSpec as P

kerr_scale = 0.1
MESH = pl.DeviceIdType.MESH
f32 = jnp.float32
bf16 = jnp.bfloat16


def split_table(table):
    high = table.astype(np.float32).astype(bf16)
    low = (table - high.astype(np.float64)).astype(np.float32).astype(bf16)
    return np.stack([np.asarray(high), np.asarray(low)])


def real_form(size):
    turns = np.outer(np.arange(size), np.arange(size)) % size
    angle = turns * (2.0 * math.pi / size)
    cosine, sine = np.cos(angle), np.sin(angle)
    return np.block([[cosine, sine], [-sine, cosine]])


def make_tables(outer, total):
    left, right = real_form(outer), real_form(128)
    turns = np.outer(np.arange(outer), np.arange(128)) % total
    angle = turns * (2.0 * math.pi / total)
    twist = np.stack([np.cos(angle), -np.sin(angle)]).astype(np.float32)
    return (
        split_table(left),
        split_table(left.T / total),
        split_table(right.T),
        split_table(right),
        twist,
    )


def halves(value):
    high = value.astype(bf16)
    return high, (value - high.astype(f32)).astype(bf16)


def mm(a, b):
    return jnp.dot(a, b, preferred_element_type=f32)


def left_dot(table, value):
    high, low = halves(value)
    return mm(table[0], high) + (mm(table[0], low) + mm(table[1], high))


def right_dot(value, table):
    high, low = halves(value)
    return mm(high, table[0]) + (mm(low, table[0]) + mm(high, table[1]))


def kernel(
    sizes, coeffs, pairs, one_left, one_right, x, target, margin,
    left_f_hbm, left_i_hbm, right_f_hbm, right_i_hbm, twist_hbm, out,
    left_f, left_i, right_f, right_i, twist, phase_tab,
    rows_in, send_z, kb, t1, t2, mg, mg_s, prods, coup, grad_pair, moved, cots, grads, rows_back, send_out,
    table_sem, own_sem, in_s, in_r, mg_ss, mg_r, t1_s, t1_r, t2_s, t2_r, kb_s, kb_r, gb_s, gb_r, out_s, out_r,
):
    Dt, Dm, B, Bl, ml, M, A, Al, As, Ak, J, total = sizes
    me_t = lax.axis_index("tm")
    me_m = lax.axis_index("mode")
    tm_peers = [lax.rem(me_t + d, Dt) for d in range(1, Dt)]
    mode_peers = [lax.rem(me_m + d, Dm) for d in range(1, Dm)]

    def remote(src, dst, send, recv, axis, peer):
        return pltpu.make_async_remote_copy(
            src_ref=src, dst_ref=dst, send_sem=send, recv_sem=recv, device_id={axis: peer}, device_id_type=MESH
        )

    barrier = pltpu.get_barrier_semaphore()
    for peer in tm_peers:
        pl.semaphore_signal(barrier, inc=1, device_id={"tm": peer}, device_id_type=MESH)
    for peer in mode_peers:
        pl.semaphore_signal(barrier, inc=1, device_id={"mode": peer}, device_id_type=MESH)
    pl.semaphore_wait(barrier, Dt + Dm - 2)

    sends = []
    owns = {}
    own_count = [0]

    def go(src, dst, send, recv, axis, peer):
        copy = remote(src, dst, send, recv, axis, peer)
        copy.start()
        sends.append(copy)

    def own(name, src, dst):
        copy = pltpu.make_async_copy(src, dst, own_sem.at[own_count[0]])
        own_count[0] += 1
        copy.start()
        owns[name] = copy

    def target_part(i):
        if (As * ml) % 8 == 0:
            return target.at[:, :, pl.ds(pl.multiple_of(i * (As * ml), 8), As * ml), :]
        return target.at[i]

    for b in range(Bl):
        for peer in tm_peers:
            go(x.at[:, peer * Bl + b], rows_in.at[b, me_t], in_s.at[b, peer], in_r.at[b, me_t], "tm", peer)
        own(("in", b), x.at[:, me_t * Bl + b], rows_in.at[b, me_t])
    for peer in mode_peers:
        go(margin, mg.at[me_m], mg_ss.at[peer], mg_r.at[me_m], "mode", peer)
    own("mg", margin, mg.at[me_m])
    for peer in mode_peers:
        go(target_part(peer), t1.at[me_m], t1_s.at[peer], t1_r.at[me_m], "mode", peer)
    own("t1", target_part(me_m), t1.at[me_m])
    table_copies = []
    for spot, (src, dst) in enumerate(
        ((left_f_hbm, left_f), (left_i_hbm, left_i), (right_f_hbm, right_f), (right_i_hbm, right_i), (twist_hbm, twist))
    ):
        copy = pltpu.make_async_copy(src, dst, table_sem.at[spot])
        copy.start()
        table_copies.append(copy)

    low_digit = lax.broadcasted_iota(jnp.int32, (A, 128), 0)
    high_digit = lax.broadcasted_iota(jnp.int32, (A, 128), 1)
    frequency = low_digit + A * high_digit
    signed = jnp.where(frequency < total // 2, frequency, frequency - total).astype(f32)
    omega = signed * (8.0 / total)
    for m in range(ml):
        phase = (
            coeffs[m, 0] * omega + coeffs[m, 1] * (omega * omega) / 2.0 + coeffs[m, 2] * (omega * omega * omega) / 6.0
        )
        phase_tab[0, m * A : (m + 1) * A, :] = jnp.cos(phase)
        phase_tab[1, m * A : (m + 1) * A, :] = jnp.sin(phase)
    for copy in table_copies:
        copy.wait()

    def disperse(stacked, direction):
        spun = left_dot(left_f, stacked)
        tw_r, tw_i = twist[0], twist[1]
        blocks = []
        for m in range(ml):
            re = spun[:A, m * 128 : (m + 1) * 128]
            im = spun[A:, m * 128 : (m + 1) * 128]
            blocks.append(jnp.concatenate([re * tw_r - im * tw_i, re * tw_i + im * tw_r], axis=1))
        spectrum = right_dot(jnp.concatenate(blocks, axis=0), right_f)
        re, im = spectrum[:, :128], spectrum[:, 128:]
        cosine = phase_tab[0]
        sine = phase_tab[1] * direction
        turned = jnp.concatenate([re * cosine - im * sine, re * sine + im * cosine], axis=1)
        back = right_dot(turned, right_i)
        real_rows, imag_rows = [], []
        for m in range(ml):
            re = back[m * A : (m + 1) * A, :128]
            im = back[m * A : (m + 1) * A, 128:]
            real_rows.append(re * tw_r + im * tw_i)
            imag_rows.append(im * tw_r - re * tw_i)
        joined = jnp.concatenate(
            [jnp.concatenate(real_rows, axis=1), jnp.concatenate(imag_rows, axis=1)], axis=0
        )
        return left_dot(left_i, joined)

    for b in range(Bl):
        owns[("in", b)].wait()
        for peer in tm_peers:
            remote(x.at[:, b], rows_in.at[b, peer], in_s.at[b, peer], in_r.at[b, peer], "tm", peer).wait_recv()
        stacked = jnp.concatenate(
            [
                jnp.concatenate(
                    [rows_in[b, j, ri, pl.ds(m, Al, stride=ml), :] for ri in range(2) for j in range(Dt)], axis=0
                )
                for m in range(ml)
            ],
            axis=1,
        )
        result = disperse(stacked, 1.0)
        for i in range(Dm):
            for m in range(ml):
                for ri in range(2):
                    for j in range(Dt):
                        row = ri * A + j * Al + i * As
                        send_z[i, b, m, ri, j * As : (j + 1) * As, :] = result[row : row + As, m * 128 : (m + 1) * 128]
        for peer in mode_peers:
            go(send_z.at[peer, b], kb[b].at[pl.ds(me_m * ml, ml)], kb_s.at[b, peer], kb_r.at[b, me_m], "mode", peer)
        own(("kb", b), send_z.at[me_m, b], kb[b].at[pl.ds(me_m * ml, ml)])

    owns["t1"].wait()
    for peer in mode_peers:
        remote(target_part(0), t1.at[peer], t1_s.at[peer], t1_r.at[peer], "mode", peer).wait_recv()
    for peer in tm_peers:
        go(t1.at[:, :, pl.ds(peer * Bl, Bl)], t2.at[me_t], t2_s.at[peer], t2_r.at[me_t], "tm", peer)
    own("t2", t1.at[:, :, pl.ds(me_t * Bl, Bl)], t2.at[me_t])
    owns["mg"].wait()
    for peer in mode_peers:
        remote(margin, mg.at[peer], mg_ss.at[peer], mg_r.at[peer], "mode", peer).wait_recv()
    own("mgs", mg, mg_s)
    owns["mgs"].wait()
    owns["t2"].wait()
    for peer in tm_peers:
        remote(
            t1.at[:, :, pl.ds(0, Bl)], t2.at[peer], t2_s.at[peer], t2_r.at[peer], "tm", peer
        ).wait_recv()

    zero = jnp.zeros((Ak, 128), f32)

    def weight(p, n, j):
        return mg_s[p // ml, lax.rem(p, ml), n * J + j]

    for b in range(Bl):
        owns[("kb", b)].wait()
        for peer in mode_peers:
            remote(
                send_z.at[0, b], kb[b].at[pl.ds(peer * ml, ml)], kb_s.at[b, peer], kb_r.at[b, peer], "mode", peer
            ).wait_recv()

        @pl.loop(0, J)
        def _(j):
            first, second = pairs[j, 0], pairs[j, 1]
            ar, ai = kb[b][first, 0], kb[b][first, 1]
            br, bi = kb[b][second, 0], kb[b][second, 1]
            prods[j, 0] = ar * br - ai * bi
            prods[j, 1] = ar * bi + ai * br

        @pl.loop(0, M)
        def _(p):
            def inner(step, carry):
                kr, ki = carry
                sums = [zero] * 4
                for j in range(J):
                    pr, pi = prods[j, 0], prods[j, 1]
                    for s in range(2):
                        w = weight(p, step * 2 + s, j)
                        sums[2 * s] = sums[2 * s] + w * pr
                        sums[2 * s + 1] = sums[2 * s + 1] + w * pi
                for s in range(2):
                    n = step * 2 + s
                    cr, ci = sums[2 * s], sums[2 * s + 1]
                    coup[p * M + n, 0] = cr
                    coup[p * M + n, 1] = ci
                    ur, ui = kb[b][n, 0], kb[b][n, 1]
                    kr = kr + (cr * ur + ci * ui)
                    ki = ki + (ci * ur - cr * ui)
                return kr, ki

            kr, ki = lax.fori_loop(0, M // 2, inner, (zero, zero))
            owner, local = p // ml, lax.rem(p, ml)
            wanted = [
                jnp.concatenate(
                    [t2[j, owner, ri, b, pl.ds(local, As, stride=ml), :] for j in range(Dt)], axis=0
                )
                for ri in range(2)
            ]
            cots[p, 0] = 2.0 * (kb[b][p, 0] - kerr_scale * ki - wanted[0])
            cots[p, 1] = 2.0 * (kb[b][p, 1] + kerr_scale * kr - wanted[1])

        @pl.loop(0, M)
        def _(n):
            ur, ui = kb[b][n, 0], kb[b][n, 1]

            def inner(p, carry):
                gr, gi = carry
                er, ei = kerr_scale * cots[p, 1], -kerr_scale * cots[p, 0]
                cr, ci = coup[p * M + n, 0], coup[p * M + n, 1]
                gr = gr + (er * cr + ei * ci)
                gi = gi + (er * ci - ei * cr)
                coup[p * M + n, 0] = er * ur - ei * ui
                coup[p * M + n, 1] = er * ui + ei * ur
                return gr, gi

            gr, gi = lax.fori_loop(0, M, inner, (cots[n, 0], cots[n, 1]))
            grads[b, n, 0] = gr
            grads[b, n, 1] = gi

        @pl.loop(0, J // 4)
        def _(quad):
            def outer(p, carry):
                sums = list(carry)
                for n in range(M):
                    sr, si = coup[p * M + n, 0], coup[p * M + n, 1]
                    for s in range(4):
                        w = weight(p, n, quad * 4 + s)
                        sums[2 * s] = sums[2 * s] + w * sr
                        sums[2 * s + 1] = sums[2 * s + 1] + w * si
                return tuple(sums)

            sums = lax.fori_loop(0, M, outer, (zero,) * 8)
            for s in range(4):
                grad_pair[quad * 4 + s, 0] = sums[2 * s]
                grad_pair[quad * 4 + s, 1] = sums[2 * s + 1]

        @pl.loop(0, J)
        def _(j):
            gr, gi = grad_pair[j, 0], grad_pair[j, 1]
            for side, other in ((0, 1), (1, 0)):
                vr, vi = kb[b][pairs[j, other], 0], kb[b][pairs[j, other], 1]
                moved[side, j, 0] = vr * gr + vi * gi
                moved[side, j, 1] = vr * gi - vi * gr

        @pl.loop(0, M)
        def _(n):
            gr, gi = grads[b, n, 0], grads[b, n, 1]
            for j in range(J):
                for side, table in ((0, one_left), (1, one_right)):
                    w = table[j, n]
                    gr = gr + w * moved[side, j, 0]
                    gi = gi + w * moved[side, j, 1]
            grads[b, n, 0] = gr
            grads[b, n, 1] = gi

        for peer in mode_peers:
            go(grads.at[b, pl.ds(peer * ml, ml)], rows_back.at[b, me_m], gb_s.at[b, peer], gb_r.at[b, me_m], "mode", peer)
        own(("gb", b), grads.at[b, pl.ds(me_m * ml, ml)], rows_back.at[b, me_m])

    for b in range(Bl):
        owns[("gb", b)].wait()
        for peer in mode_peers:
            remote(
                grads.at[b, pl.ds(0, ml)], rows_back.at[b, peer], gb_s.at[b, peer], gb_r.at[b, peer], "mode", peer
            ).wait_recv()
        stacked = jnp.concatenate(
            [
                jnp.concatenate(
                    [
                        rows_back[b, i, m, ri, j * As : (j + 1) * As, :]
                        for ri in range(2)
                        for j in range(Dt)
                        for i in range(Dm)
                    ],
                    axis=0,
                )
                for m in range(ml)
            ],
            axis=1,
        )
        result = disperse(stacked, -1.0)
        for j in range(Dt):
            for ri in range(2):
                for m in range(ml):
                    row = ri * A + j * Al
                    send_out[j, b, ri, pl.ds(m, Al, stride=ml), :] = result[row : row + Al, m * 128 : (m + 1) * 128]
        for peer in tm_peers:
            go(send_out.at[peer, b], out.at[:, me_t * Bl + b], out_s.at[b, peer], out_r.at[b, me_t], "tm", peer)
        own(("out", b), send_out.at[me_t, b], out.at[:, me_t * Bl + b])
    for b in range(Bl):
        owns[("out", b)].wait()
        for peer in tm_peers:
            remote(
                send_out.at[0, b], out.at[:, peer * Bl + b], out_s.at[b, peer], out_r.at[b, peer], "tm", peer
            ).wait_recv()
    for copy in sends:
        copy.wait_send()


def on_device(Dm, Dt, input_field, target_field, margin, pair_index, mode_beta, segment_kind):
    _, B, ml, Tl = input_field.shape
    M, J = margin.shape[1], margin.shape[2]
    total = Tl * Dt
    A = total // 128
    Al = Tl // 128
    Bl = B // Dt
    As = Al // Dm
    Ak = As * Dt
    coeffs = lax.dynamic_index_in_dim(mode_beta, segment_kind[0], 0, keepdims=False)
    columns = lax.broadcasted_iota(jnp.int32, (J, M), 1)
    one_left = (pair_index[:, 0:1] == columns).astype(f32)
    one_right = (pair_index[:, 1:2] == columns).astype(f32)

    def by_rows(values):
        return values.reshape(2, B, ml, Al, 128).transpose(0, 1, 3, 2, 4).reshape(2, B, Al * ml, 128)

    x = by_rows(input_field)
    target = by_rows(target_field)
    if (As * ml) % 8:
        target = target.reshape(2, B, Dm, As * ml, 128).transpose(2, 0, 1, 3, 4)
    tables = make_tables(A, total)
    sizes = (Dt, Dm, B, Bl, ml, M, A, Al, As, Ak, J, total)
    vm = lambda *shape: pltpu.VMEM(shape, f32)
    dma = lambda *shape: pltpu.SemaphoreType.DMA(shape)
    anyspace = pl.BlockSpec(memory_space=pl.ANY)
    smem = pl.BlockSpec(memory_space=pltpu.SMEM)
    vmem = pl.BlockSpec(memory_space=pltpu.VMEM)
    out = pl.pallas_call(
        functools.partial(kernel, sizes),
        out_shape=jax.ShapeDtypeStruct((2, B, Al * ml, 128), f32),
        in_specs=[smem] * 4 + [anyspace, anyspace, vmem] + [anyspace] * 5,
        out_specs=vmem,
        scratch_shapes=[pltpu.VMEM(t.shape, bf16) for t in tables[:4]]
        + [
            vm(2, A, 128),
            vm(2, ml * A, 128),
            vm(Bl, Dt, 2, Al * ml, 128),
            vm(Dm, Bl, ml, 2, Ak, 128),
            [vm(M, 2, Ak, 128) for _ in range(Bl)],
            vm(Dm, 2, B, As * ml, 128),
            vm(Dt, Dm, 2, Bl, As * ml, 128),
            vm(Dm, ml, M * J),
            pltpu.SMEM((Dm, ml, M * J), f32),
            vm(J, 2, Ak, 128),
            vm(M * M, 2, Ak, 128),
            vm(J, 2, Ak, 128),
            vm(2, J, 2, Ak, 128),
            vm(M, 2, Ak, 128),
            vm(Bl, M, 2, Ak, 128),
            vm(Bl, Dm, ml, 2, Ak, 128),
            vm(Dt, Bl, 2, Al * ml, 128),
            dma(5),
            dma(4 * Bl + 4),
            dma(Bl, Dt), dma(Bl, Dt),
            dma(Dm), dma(Dm),
            dma(Dm), dma(Dm),
            dma(Dt), dma(Dt),
            dma(Bl, Dm), dma(Bl, Dm),
            dma(Bl, Dm), dma(Bl, Dm),
            dma(Bl, Dt), dma(Bl, Dt),
        ],
        compiler_params=pltpu.CompilerParams(collective_id=0, has_side_effects=True, vmem_limit_bytes=62 * 1024 * 1024),
    )(coeffs, pair_index, one_left, one_right, x, target, margin.reshape(ml, M * J), *[jnp.asarray(t) for t in tables])
    return out.reshape(2, B, Al, ml, 128).transpose(0, 1, 3, 2, 4).reshape(2, B, ml, Tl)


def solution(mesh):
    return jax.shard_map(
        functools.partial(on_device, mesh.shape["mode"], mesh.shape["tm"]),
        mesh=mesh,
        in_specs=(
            P(None, "dp", "mode", "tm"),
            P(None, "dp", "mode", "tm"),
            P("mode", None, None),
            P(),
            P(None, "mode", None),
            P(),
        ),
        out_specs=P(None, "dp", "mode", "tm"),
        check_vma=False,
    )
```

profile of v0, /device:TPU:1, one launch (start us, length us, event | category | flops | bytes accessed | tf_op | source)
XLA Modules:
  0.0 64.8 jit_solution(5383568186620165396)
XLA Ops:
  0.0 0.0 copy-start
  0.7 0.0 copy-start.1
  0.7 0.7 %copy-done.1 = f32[2,8,16]{2,1,0:T(8,128)S(1)} copy-done((f32[2,8,16]{2,1,0:T(8,128)S(1)}, f32[2,8,16]{2,1,0:T(8,128)}, u32[]{:S(2)}) %copy-start.1) | copy-done | bytes 1048
  1.4 0.0 copy-start.2
  1.4 0.6 reshape.25.margin
  2.0 0.1 copy-done.2
  2.0 0.0 copy-done
  2.0 0.1 constant_dynamic-slice_fusion
  2.1 0.7 %copy.12 = f32[1,2,3]{2,1,0:T(2,128)} copy(f32[1,2,3]{0,1,2:T(2,128)S(1)} %constant_dynamic-slice_fusion) | data formatting | bytes 48 | tf_op jit(solution)/shard_map/jit(dynamic_index_in_dim)/dynamic_slice | solution.py:366
  2.8 0.7 %copy.15.pairs = s32[16,2]{1,0:T(8,128)} copy(s32[16,2]{0,1:T(2,128)S(1)} %copy-done.2) | data formatting | bytes 256 | tf_op args[3]
  3.5 0.7 %fusion = (f32[16,8]{1,0:T(8,128)}, f32[16,8]{1,0:T(8,128)}) fusion(s32[16]{0:T(128)S(1)} %get-tuple-element.6, s32[16]{0:T(128)S(1)} %get-tuple-element.5), kind=kLoop, calls=%fused_computation.2 | loop fusion | flops 512 | bytes 1152 | tf_op jit(solution)/shard_map/convert_element_type | solution.py:368
  4.2 58.7 %shard_map.109 = f32[2,8,64,128]{3,2,1,0:T(8,128)} custom-call(f32[2,3]{1,0:T(2,128)} %bitcast.27, s32[16,2]{1,0:T(8,128)} %copy.15.pairs, f32[16,8]{1,0:T(8,128)} %get-tuple-element.7.one_left, f32[16,8]{1,0:T(8,128)} %get-tuple-element.8.one_right, f32[2,8,64,128]{3,2,1,0:T(8,128)} %bitcast.25, f32[2,8,64,128]{3,2,1,0:T(8,128)} %bitcast.26, ...), custom_call_target="tpu_custom_call" | custom-call | tf_op jit(solution)/shard_map/pallas_call | solution.py:385
  62.9 1.9 %copy.19 = f32[2,8,2,4096]{3,2,1,0:T(2,128)} copy(f32[2,8,2,4096]{3,2,1,0:T(2,128)} %bitcast.24) | data formatting | bytes 1048576
  (1 shorter events, 0.0 us)
Async XLA Ops:
  0.0 2.0 %copy-start = (f32[1024,2,3]{0,1,2:T(2,128)S(1)}, f32[1024,2,3]{0,1,2:T(2,128)}, u32[]{:S(2)}) copy-start(f32[1024,2,3]{0,1,2:T(2,128)} %param.15) | copy-start | bytes 73732
  0.7 0.7 %copy-start.1 = (f32[2,8,16]{2,1,0:T(8,128)S(1)}, f32[2,8,16]{2,1,0:T(8,128)}, u32[]{:S(2)}) copy-start(f32[2,8,16]{2,1,0:T(8,128)} %param.13) | copy-start | bytes 3076
  1.4 0.7 %copy-start.2 = (s32[16,2]{0,1:T(2,128)S(1)}, s32[16,2]{0,1:T(2,128)}, u32[]{:S(2)}) copy-start(s32[16,2]{0,1:T(2,128)} %param.14) | copy-start | bytes 388
where the time goes:
time: 65.1 us; the launch traced here: 64.8 us
  Pallas kernels  58.7 us (90%)
  local copies, waits for them, and re-layouts  4.69 us (7%)
  between operations  0.69 us (1%)
  other arithmetic  0.66 us (1%)
    pallas_call x1, Pallas kernels, on_device(): pl.pallas_call(functools.partial(kernel, sizes), out_shape=jax.ShapeDtype...  58.7 us
    unnamed x8, local copies, waits for them, and re-layouts  3.32 us

commit v1 on v0

--- a/solution.py
+++ b/solution.py
@@ -61,18 +61,28 @@
     return mm(high, table[0]) + (mm(low, table[0]) + mm(high, table[1]))
 
 
+def farthest_first(me, count):
+    low, high = jnp.int32(0), jnp.int32(count - 1)
+    peers = []
+    for _ in range(count - 1):
+        up = (high - me >= me - low).astype(jnp.int32)
+        peers.append(up * high + (1 - up) * low)
+        high, low = high - up, low + 1 - up
+    return peers
+
+
 def kernel(
-    sizes, coeffs, pairs, one_left, one_right, x, target, margin,
+    sizes, kind, pairs, x, target, margin, beta_hbm,
     left_f_hbm, left_i_hbm, right_f_hbm, right_i_hbm, twist_hbm, out,
-    left_f, left_i, right_f, right_i, twist, phase_tab,
+    left_f, left_i, right_f, right_i, twist, beta, phase_tab,
     rows_in, send_z, kb, t1, t2, mg, mg_s, prods, coup, grad_pair, moved, cots, grads, rows_back, send_out,
     table_sem, own_sem, in_s, in_r, mg_ss, mg_r, t1_s, t1_r, t2_s, t2_r, kb_s, kb_r, gb_s, gb_r, out_s, out_r,
 ):
     Dt, Dm, B, Bl, ml, M, A, Al, As, Ak, J, total = sizes
     me_t = lax.axis_index("tm")
     me_m = lax.axis_index("mode")
-    tm_peers = [lax.rem(me_t + d, Dt) for d in range(1, Dt)]
-    mode_peers = [lax.rem(me_m + d, Dm) for d in range(1, Dm)]
+    tm_peers = farthest_first(me_t, Dt)
+    mode_peers = farthest_first(me_m, Dm)
 
     def remote(src, dst, send, recv, axis, peer):
         return pltpu.make_async_remote_copy(
@@ -101,10 +111,23 @@
         copy.start()
         owns[name] = copy
 
-    def target_part(i):
+    def target_part(i, b):
         if (As * ml) % 8 == 0:
-            return target.at[:, :, pl.ds(pl.multiple_of(i * (As * ml), 8), As * ml), :]
-        return target.at[i]
+            return target.at[:, :, b, pl.ds(pl.multiple_of(i * (As * ml), 8), As * ml), :]
+        return target.at[i, :, :, b]
+
+    def target_first_leg(b):
+        for peer in mode_peers:
+            go(target_part(peer, b), t1[b].at[me_m], t1_s.at[b, peer], t1_r.at[b, me_m], "mode", peer)
+        own(("t1", b), target_part(me_m, b), t1[b].at[me_m])
+
+    def target_second_leg(b):
+        owns[("t1", b)].wait()
+        for peer in mode_peers:
+            remote(target_part(0, b), t1[b].at[peer], t1_s.at[b, peer], t1_r.at[b, peer], "mode", peer).wait_recv()
+        for peer in tm_peers:
+            go(t1[b].at[:, :, peer], t2[b].at[me_t], t2_s.at[b, peer], t2_r.at[b, me_t], "tm", peer)
+        own(("t2", b), t1[b].at[:, :, me_t], t2[b].at[me_t])
 
     for b in range(Bl):
         for peer in tm_peers:
@@ -113,17 +136,17 @@
     for peer in mode_peers:
         go(margin, mg.at[me_m], mg_ss.at[peer], mg_r.at[me_m], "mode", peer)
     own("mg", margin, mg.at[me_m])
-    for peer in mode_peers:
-        go(target_part(peer), t1.at[me_m], t1_s.at[peer], t1_r.at[me_m], "mode", peer)
-    own("t1", target_part(me_m), t1.at[me_m])
+    target_first_leg(0)
     table_copies = []
     for spot, (src, dst) in enumerate(
-        ((left_f_hbm, left_f), (left_i_hbm, left_i), (right_f_hbm, right_f), (right_i_hbm, right_i), (twist_hbm, twist))
+        ((left_f_hbm, left_f), (left_i_hbm, left_i), (right_f_hbm, right_f), (right_i_hbm, right_i), (twist_hbm, twist), (beta_hbm, beta))
     ):
         copy = pltpu.make_async_copy(src, dst, table_sem.at[spot])
         copy.start()
         table_copies.append(copy)
 
+    for copy in table_copies:
+        copy.wait()
     low_digit = lax.broadcasted_iota(jnp.int32, (A, 128), 0)
     high_digit = lax.broadcasted_iota(jnp.int32, (A, 128), 1)
     frequency = low_digit + A * high_digit
@@ -131,13 +154,12 @@
     omega = signed * (8.0 / total)
     for m in range(ml):
         phase = (
-            coeffs[m, 0] * omega + coeffs[m, 1] * (omega * omega) / 2.0 + coeffs[m, 2] * (omega * omega * omega) / 6.0
+            beta[0, m, kind[0]] * omega
+            + beta[1, m, kind[0]] * (omega * omega) / 2.0
+            + beta[2, m, kind[0]] * (omega * omega * omega) / 6.0
         )
         phase_tab[0, m * A : (m + 1) * A, :] = jnp.cos(phase)
         phase_tab[1, m * A : (m + 1) * A, :] = jnp.sin(phase)
-    for copy in table_copies:
-        copy.wait()
-
     def disperse(stacked, direction):
         spun = left_dot(left_f, stacked)
         tw_r, tw_i = twist[0], twist[1]
@@ -186,23 +208,16 @@
         for peer in mode_peers:
             go(send_z.at[peer, b], kb[b].at[pl.ds(me_m * ml, ml)], kb_s.at[b, peer], kb_r.at[b, me_m], "mode", peer)
         own(("kb", b), send_z.at[me_m, b], kb[b].at[pl.ds(me_m * ml, ml)])
-
-    owns["t1"].wait()
-    for peer in mode_peers:
-        remote(target_part(0), t1.at[peer], t1_s.at[peer], t1_r.at[peer], "mode", peer).wait_recv()
-    for peer in tm_peers:
-        go(t1.at[:, :, pl.ds(peer * Bl, Bl)], t2.at[me_t], t2_s.at[peer], t2_r.at[me_t], "tm", peer)
-    own("t2", t1.at[:, :, pl.ds(me_t * Bl, Bl)], t2.at[me_t])
+        if b + 1 < Bl:
+            target_first_leg(b + 1)
+        if b == 0:
+            target_second_leg(0)
+
     owns["mg"].wait()
     for peer in mode_peers:
         remote(margin, mg.at[peer], mg_ss.at[peer], mg_r.at[peer], "mode", peer).wait_recv()
     own("mgs", mg, mg_s)
     owns["mgs"].wait()
-    owns["t2"].wait()
-    for peer in tm_peers:
-        remote(
-            t1.at[:, :, pl.ds(0, Bl)], t2.at[peer], t2_s.at[peer], t2_r.at[peer], "tm", peer
-        ).wait_recv()
 
     zero = jnp.zeros((Ak, 128), f32)
 
@@ -215,10 +230,13 @@
             remote(
                 send_z.at[0, b], kb[b].at[pl.ds(peer * ml, ml)], kb_s.at[b, peer], kb_r.at[b, peer], "mode", peer
             ).wait_recv()
+        owns[("t2", b)].wait()
+        for peer in tm_peers:
+            remote(t1[b].at[:, :, 0], t2[b].at[peer], t2_s.at[b, peer], t2_r.at[b, peer], "tm", peer).wait_recv()
 
         @pl.loop(0, J)
         def _(j):
-            first, second = pairs[j, 0], pairs[j, 1]
+            first, second = pairs[0, j], pairs[1, j]
             ar, ai = kb[b][first, 0], kb[b][first, 1]
             br, bi = kb[b][second, 0], kb[b][second, 1]
             prods[j, 0] = ar * br - ai * bi
@@ -249,7 +267,7 @@
             owner, local = p // ml, lax.rem(p, ml)
             wanted = [
                 jnp.concatenate(
-                    [t2[j, owner, ri, b, pl.ds(local, As, stride=ml), :] for j in range(Dt)], axis=0
+                    [t2[b][j, owner, ri, pl.ds(local, As, stride=ml), :] for j in range(Dt)], axis=0
                 )
                 for ri in range(2)
             ]
@@ -295,7 +313,7 @@
         def _(j):
             gr, gi = grad_pair[j, 0], grad_pair[j, 1]
             for side, other in ((0, 1), (1, 0)):
-                vr, vi = kb[b][pairs[j, other], 0], kb[b][pairs[j, other], 1]
+                vr, vi = kb[b][pairs[other, j], 0], kb[b][pairs[other, j], 1]
                 moved[side, j, 0] = vr * gr + vi * gi
                 moved[side, j, 1] = vr * gi - vi * gr
 
@@ -303,8 +321,8 @@
         def _(n):
             gr, gi = grads[b, n, 0], grads[b, n, 1]
             for j in range(J):
-                for side, table in ((0, one_left), (1, one_right)):
-                    w = table[j, n]
+                for side in range(2):
+                    w = (pairs[side, j] == n).astype(f32)
                     gr = gr + w * moved[side, j, 0]
                     gi = gi + w * moved[side, j, 1]
             grads[b, n, 0] = gr
@@ -312,6 +330,8 @@
 
         for peer in mode_peers:
             go(grads.at[b, pl.ds(peer * ml, ml)], rows_back.at[b, me_m], gb_s.at[b, peer], gb_r.at[b, me_m], "mode", peer)
+        if b + 1 < Bl:
+            target_second_leg(b + 1)
         own(("gb", b), grads.at[b, pl.ds(me_m * ml, ml)], rows_back.at[b, me_m])
 
     for b in range(Bl):
@@ -363,18 +383,13 @@
     Bl = B // Dt
     As = Al // Dm
     Ak = As * Dt
-    coeffs = lax.dynamic_index_in_dim(mode_beta, segment_kind[0], 0, keepdims=False)
-    columns = lax.broadcasted_iota(jnp.int32, (J, M), 1)
-    one_left = (pair_index[:, 0:1] == columns).astype(f32)
-    one_right = (pair_index[:, 1:2] == columns).astype(f32)
-
     def by_rows(values):
         return values.reshape(2, B, ml, Al, 128).transpose(0, 1, 3, 2, 4).reshape(2, B, Al * ml, 128)
 
     x = by_rows(input_field)
-    target = by_rows(target_field)
+    target = by_rows(target_field).reshape(2, Dt, Bl, Al * ml, 128)
     if (As * ml) % 8:
-        target = target.reshape(2, B, Dm, As * ml, 128).transpose(2, 0, 1, 3, 4)
+        target = target.reshape(2, Dt, Bl, Dm, As * ml, 128).transpose(3, 0, 1, 2, 4, 5)
     tables = make_tables(A, total)
     sizes = (Dt, Dm, B, Bl, ml, M, A, Al, As, Ak, J, total)
     vm = lambda *shape: pltpu.VMEM(shape, f32)
@@ -385,17 +400,18 @@
     out = pl.pallas_call(
         functools.partial(kernel, sizes),
         out_shape=jax.ShapeDtypeStruct((2, B, Al * ml, 128), f32),
-        in_specs=[smem] * 4 + [anyspace, anyspace, vmem] + [anyspace] * 5,
+        in_specs=[smem] * 2 + [anyspace, anyspace, vmem] + [anyspace] * 6,
         out_specs=vmem,
         scratch_shapes=[pltpu.VMEM(t.shape, bf16) for t in tables[:4]]
         + [
             vm(2, A, 128),
+            pltpu.SMEM((3, ml, mode_beta.shape[0]), f32),
             vm(2, ml * A, 128),
             vm(Bl, Dt, 2, Al * ml, 128),
             vm(Dm, Bl, ml, 2, Ak, 128),
             [vm(M, 2, Ak, 128) for _ in range(Bl)],
-            vm(Dm, 2, B, As * ml, 128),
-            vm(Dt, Dm, 2, Bl, As * ml, 128),
+            [vm(Dm, 2, Dt, As * ml, 128) for _ in range(Bl)],
+            [vm(Dt, Dm, 2, As * ml, 128) for _ in range(Bl)],
             vm(Dm, ml, M * J),
             pltpu.SMEM((Dm, ml, M * J), f32),
             vm(J, 2, Ak, 128),
@@ -406,18 +422,18 @@
             vm(Bl, M, 2, Ak, 128),
             vm(Bl, Dm, ml, 2, Ak, 128),
             vm(Dt, Bl, 2, Al * ml, 128),
-            dma(5),
-            dma(4 * Bl + 4),
+            dma(6),
+            dma(6 * Bl + 2),
             dma(Bl, Dt), dma(Bl, Dt),
             dma(Dm), dma(Dm),
-            dma(Dm), dma(Dm),
-            dma(Dt), dma(Dt),
+            dma(Bl, Dm), dma(Bl, Dm),
+            dma(Bl, Dt), dma(Bl, Dt),
             dma(Bl, Dm), dma(Bl, Dm),
             dma(Bl, Dm), dma(Bl, Dm),
             dma(Bl, Dt), dma(Bl, Dt),
         ],
         compiler_params=pltpu.CompilerParams(collective_id=0, has_side_effects=True, vmem_limit_bytes=62 * 1024 * 1024),
-    )(coeffs, pair_index, one_left, one_right, x, target, margin.reshape(ml, M * J), *[jnp.asarray(t) for t in tables])
+    )(segment_kind, pair_index.T, x, target, margin.reshape(ml, M * J), mode_beta.transpose(2, 1, 0), *[jnp.asarray(t) for t in tables])
     return out.reshape(2, B, Al, ml, 128).transpose(0, 1, 3, 2, 4).reshape(2, B, ml, Tl)
 
 

time: 65.1 us -> 58.6 us (0.900)
  Pallas kernels: 58.7 us -> 55.1 us
  local copies, waits for them, and re-layouts: 4.69 us -> 2.56 us
  other arithmetic: 0.66 us -> 0 us
    pallas_call x1, Pallas kernels: 58.7 us -> 55.1 us  [on_device(): pl.pallas_call(functools.partial(kernel, sizes), out_shape=jax.ShapeDtype...]
    unnamed x8 -> x3, local copies, waits for them, and re-layouts: 3.32 us -> 1.92 us
    dynamic_slice x2 -> x0, local copies, waits for them, and re-layouts: 0.76 us -> none  [on_device(): lax.dynamic_index_in_dim(mode_beta, segment_kind[0], 0, keepdims=False)]
    convert_element_type x1 -> x0, other arithmetic: 0.66 us -> none  [on_device(): one_left = (pair_index[:, 0:1] == columns).astype(f32)]
where the time goes in v1:
time: 58.6 us; the launch traced here: 58.4 us
  Pallas kernels  55.1 us (94%)
  local copies, waits for them, and re-layouts  2.56 us (4%)
  between operations  0.68 us (1%)
    pallas_call x1, Pallas kernels, on_device(): pl.pallas_call(functools.partial(kernel, sizes), out_shape=jax.ShapeDtype...  55.1 us
    unnamed x3, local copies, waits for them, and re-layouts  1.92 us

profile of v1, /device:TPU:1, one launch (start us, length us, event | category | flops | bytes accessed | tf_op | source)
XLA Modules:
  0.0 58.4 jit_solution(7393460279061344686)
XLA Ops:
  0.0 0.0 copy-start
  0.7 0.0 copy-done
  0.7 0.6 %reshape.21.margin = f32[2,128]{1,0:T(2,128)} reshape(f32[2,8,16]{2,1,0:T(8,128)S(1)} %copy-done) | data formatting | bytes 2048 | tf_op jit(solution)/shard_map/reshape | solution.py:436
  1.3 55.1 %shard_map.109 = f32[2,8,64,128]{3,2,1,0:T(8,128)} custom-call(s32[1]{0:T(128)S(6)} %copy.16.kind, s32[2,16]{1,0:T(2,128)} %bitcast.21, f32[2,8,64,128]{3,2,1,0:T(8,128)} %bitcast.18, f32[2,4,2,64,128]{4,3,2,1,0:T(8,128)} %bitcast.19, f32[2,128]{1,0:T(2,128)} %reshape.21.margin, f32[3,2,1024]{2,1,0:T(2,128)} %bitcast.20, ...), custom_call_target="tpu_custom_call" | custom-call | tf_op jit(solution)/shard_map/pallas_call | solution.py:400
  56.5 1.9 %copy.17 = f32[2,8,2,4096]{3,2,1,0:T(2,128)} copy(f32[2,8,2,4096]{3,2,1,0:T(2,128)} %bitcast.17) | data formatting | bytes 1048576
Async XLA Ops:
  0.0 0.7 %copy-start = (f32[2,8,16]{2,1,0:T(8,128)S(1)}, f32[2,8,16]{2,1,0:T(8,128)}, u32[]{:S(2)}) copy-start(f32[2,8,16]{2,1,0:T(8,128)} %param.13) | copy-start | bytes 3076

commit v2 on v1

--- a/solution.py
+++ b/solution.py
@@ -263,7 +263,7 @@
                     ki = ki + (ci * ur - cr * ui)
                 return kr, ki
 
-            kr, ki = lax.fori_loop(0, M // 2, inner, (zero, zero))
+            kr, ki = lax.fori_loop(0, M // 2, inner, (zero, zero), unroll=4)
             owner, local = p // ml, lax.rem(p, ml)
             wanted = [
                 jnp.concatenate(
@@ -288,7 +288,7 @@
                 coup[p * M + n, 1] = er * ui + ei * ur
                 return gr, gi
 
-            gr, gi = lax.fori_loop(0, M, inner, (cots[n, 0], cots[n, 1]))
+            gr, gi = lax.fori_loop(0, M, inner, (cots[n, 0], cots[n, 1]), unroll=8)
             grads[b, n, 0] = gr
             grads[b, n, 1] = gi
 

time: 58.6 us -> 57.4 us (0.980)
  Pallas kernels: 55.1 us -> 53.6 us
    pallas_call x1, Pallas kernels: 55.1 us -> 53.6 us  [on_device(): pl.pallas_call(functools.partial(kernel, sizes), out_shape=jax.ShapeDtype...]
where the time goes in v2:
time: 57.4 us; the launch traced here: 56.9 us
  Pallas kernels  53.6 us (93%)
  local copies, waits for them, and re-layouts  2.56 us (4%)
  between operations  0.68 us (1%)
    pallas_call x1, Pallas kernels, on_device(): pl.pallas_call(functools.partial(kernel, sizes), out_shape=jax.ShapeDtype...  53.6 us
    unnamed x3, local copies, waits for them, and re-layouts  1.92 us

profile of v2, /device:TPU:1, one launch (start us, length us, event | category | flops | bytes accessed | tf_op | source)
XLA Modules:
  0.0 56.9 jit_solution(15180059203204597182)
XLA Ops:
  0.0 0.0 copy-start
  0.7 0.0 copy-done
  0.7 0.6 %reshape.21.margin = f32[2,128]{1,0:T(2,128)} reshape(f32[2,8,16]{2,1,0:T(8,128)S(1)} %copy-done) | data formatting | bytes 2048 | tf_op jit(solution)/shard_map/reshape | solution.py:436
  1.3 53.6 %shard_map.109 = f32[2,8,64,128]{3,2,1,0:T(8,128)} custom-call(s32[1]{0:T(128)S(6)} %copy.16.kind, s32[2,16]{1,0:T(2,128)} %bitcast.21, f32[2,8,64,128]{3,2,1,0:T(8,128)} %bitcast.18, f32[2,4,2,64,128]{4,3,2,1,0:T(8,128)} %bitcast.19, f32[2,128]{1,0:T(2,128)} %reshape.21.margin, f32[3,2,1024]{2,1,0:T(2,128)} %bitcast.20, ...), custom_call_target="tpu_custom_call" | custom-call | tf_op jit(solution)/shard_map/pallas_call | solution.py:400
  55.0 1.9 %copy.17 = f32[2,8,2,4096]{3,2,1,0:T(2,128)} copy(f32[2,8,2,4096]{3,2,1,0:T(2,128)} %bitcast.17) | data formatting | bytes 1048576
Async XLA Ops:
  0.0 0.7 %copy-start = (f32[2,8,16]{2,1,0:T(8,128)S(1)}, f32[2,8,16]{2,1,0:T(8,128)}, u32[]{:S(2)}) copy-start(f32[2,8,16]{2,1,0:T(8,128)} %param.13) | copy-start | bytes 3076
